TPU v7x, 32 devices: a whole 2x2x4 slice. The times are simulated.
32 devices in a mesh: batch: 4 (over y, x), centre: 8 (over z, core).
Axes of the slice: x: 2, y: 2, z: 4, core: 2. Of those that a mesh axis runs over, the one named last changes fastest.
Arguments:
- pool: float32 [1024, 1024], P('batch', 'centre'), may hold values from -4.5 to 4.5
- sample_index: int32 [512], P('batch'), may hold values from 0 to 255
- targets: float32 [512, 256], P('batch'), may hold values from -6 to 6
- centres: float32 [512, 1024], P(('batch', 'centre')), may hold values from -4.5 to 4.5
- coeffs: float32 [512, 256], P(('batch', 'centre')), may hold values from -6 to 6
- eigvecs: float32 [512, 1024], P(('batch', 'centre')), may hold values from -0.75 to 0.75
- eigscale: float32 [1024], replicated, may hold values from 0.1 to 0.95
Outputs:
- new_coeffs: float32 [512, 256], P(('batch', 'centre'))
Inputs may be any that keep to these rules, and one draw needn't show every extreme that they name: `sample_index`: each batch row's sample lies in the block of 256 training samples held by its own batch group; the index counts within that block.
All inputs are finite; a program needn't handle non-finite values.
Results may differ from a plain program's by a relative error of at most 0.0003.
Values sent between devices are 32-bit elements; how exact they have to be, the bound alone decides.
A program may use at most 64 MiB of HBM per device.

v0:
```python
import jax
import jax.numpy as jnp
from jax import lax
from jax.sharding import PartitionSpec as P


def on_device(pool, sample_index, targets, centres, coeffs, eigvecs, eigscale):
    highest = lax.Precision.HIGHEST
    picked = jnp.take(pool, sample_index, axis=0)
    batch_x = lax.all_gather(picked, "centre", axis=1, tiled=True)
    row_count = batch_x.shape[0]
    n_batch = lax.axis_size("batch")
    n_centre = lax.axis_size("centre")
    own_centres = centres.shape[0]
    group_rows = own_centres * n_batch
    total_centres = group_rows * n_centre
    total_rows = row_count * n_batch
    width = batch_x.shape[1]
    inv_width = 1.0 / jnp.sqrt(jnp.float32(width))
    model_norm = 1.0 / jnp.sqrt(jnp.float32(total_centres))
    zrows = lax.all_gather(centres, "batch", axis=0, tiled=True)
    crows = lax.all_gather(coeffs, "batch", axis=0, tiled=True)
    scores = lax.dot_general(
        batch_x,
        zrows,
        (((1,), (1,)), ((), ())),
        precision=highest,
        preferred_element_type=jnp.float32,
    )
    kpiece = jnp.exp(scores * inv_width)
    partial_value = jnp.dot(kpiece, crows, precision=highest, preferred_element_type=jnp.float32)
    kernel, partial_value = (kpiece, partial_value)
    columns = (
        lax.psum_scatter(partial_value, "centre", scatter_dimension=1, tiled=True) * model_norm
    )
    col_width = columns.shape[1]
    col_offset = lax.axis_index("centre") * col_width
    own_targets = lax.dynamic_slice_in_dim(targets, col_offset, col_width, 1)
    residual = lax.all_gather(columns - own_targets, "centre", axis=1, tiled=True)
    gradient = (
        lax.psum_scatter(
            lax.dot_general(
                kernel,
                residual,
                (((0,), (0,)), ((), ())),
                precision=highest,
                preferred_element_type=jnp.float32,
            ),
            "batch",
            scatter_dimension=0,
            tiled=True,
        )
        * model_norm
    )
    local_coords = lax.dot_general(
        eigvecs,
        gradient,
        (((0,), (0,)), ((), ())),
        precision=highest,
        preferred_element_type=jnp.float32,
    )
    coords = lax.psum(local_coords, ("batch", "centre"))
    correction = jnp.dot(
        eigvecs, eigscale[:, None] * coords, precision=highest, preferred_element_type=jnp.float32
    )
    step_size = 0.5 * jnp.sqrt(jnp.float32(total_centres) / jnp.float32(total_rows))
    return coeffs - step_size * (gradient - correction)


def solution(mesh):
    return jax.shard_map(
        on_device,
        mesh=mesh,
        in_specs=(
            P("batch", "centre"),
            P("batch"),
            P("batch", None),
            P(("batch", "centre"), None),
            P(("batch", "centre"), None),
            P(("batch", "centre"), None),
            P(),
        ),
        out_specs=P(("batch", "centre"), None),
        check_vma=False,
    )
```

profile of v0, /device:TPU:0, one launch (start us, length us, event | category | flops | bytes accessed | tf_op | source)
XLA Modules:
  0.0 257.5 jit_solution(9517945055729336617)
XLA Ops:
  6.5 0.0 copy-start
  6.5 0.0 reduce-scatter.7.cloned.1.call-start
  6.5 0.7 compare_and_fusion
  7.3 0.0 copy-done.7
  7.3 9.9 %all_gather.14 = f32[64,256]{1,0:T(8,128)S(1)} all-gather(f32[16,256]{1,0:T(8,128)} %param.11), channel_id=1, replica_groups=mesh['batch'=4,'centre'=8] {'batch'}, dimensions={0}, use_global_device_ids=true | all-gather | bytes 81920 | tf_op jit(solution)/shard_map/all_gather | solution.py:22
  17.2 0.0 copy-done.4
  17.2 8.8 %all_gather.13 = f32[64,1024]{1,0:T(8,128)S(1)} all-gather(f32[16,1024]{1,0:T(8,128)S(1)} %copy-done.4), channel_id=1, replica_groups=mesh['batch'=4,'centre'=8] {'batch'}, dimensions={0}, use_global_device_ids=true | all-gather | bytes 327680 | tf_op jit(solution)/shard_map/all_gather | solution.py:21
  26.0 0.0 copy-done
  26.0 0.6 gather_fusion
  26.6 0.1 broadcast_select_fusion
  26.7 15.2 %all_gather.12 = f32[128,1024]{1,0:T(8,128)S(1)} all-gather(f32[128,128]{1,0:T(8,128)S(1)} %broadcast_select_fusion), channel_id=1, replica_groups=mesh['batch'=4,'centre'=8] {'centre'}, dimensions={1}, use_global_device_ids=true | all-gather | bytes 589824 | tf_op jit(solution)/shard_map/all_gather | solution.py:10
  41.9 0.7 fusion
  42.6 1.1 convolution_bitcast_fusion.1
  43.7 0.0 reduce-scatter.7.cloned.1.call-update
  43.7 0.0 reduce-scatter.5.cloned.1.call-start
  43.7 0.8 copy-done.5
  44.6 0.1 constant_dynamic-slice_fusion
  44.6 0.1 copy.15
  44.7 29.6 %reduce-scatter.7.cloned.1.call-done = f32[32,128]{1,0:T(8,128)} async-done(((f32[256,128]{1,0:T(8,128)}), f32[32,128]{1,0:T(8,128)}) %reduce-scatter.7.cloned.1.call-update) | async-done | bytes 16400
  74.3 0.7 fusion.6
  75.1 13.9 %all_gather.15 = f32[128,256]{0,1:T(8,128)S(1)} all-gather(f32[128,32]{0,1:T(8,128)S(1)} %fusion.6), channel_id=1, replica_groups=mesh['batch'=4,'centre'=8] {'centre'}, dimensions={1}, use_global_device_ids=true | all-gather | bytes 147456 | tf_op jit(solution)/shard_map/all_gather | solution.py:39
  89.0 0.9 fusion.10
  89.9 0.0 reduce-scatter.5.cloned.1.call-update
  89.9 0.0 all-reduce.2.cloned.1.call-start
  90.0 22.3 %reduce-scatter.5.cloned.1.call-done = f32[16,256]{1,0:T(8,128)} async-done(((f32[64,256]{1,0:T(8,128)}), f32[16,256]{1,0:T(8,128)}) %reduce-scatter.5.cloned.1.call-update) | async-done | bytes 16400 | tf_op jit(solution)/shard_map/reduce_scatter | solution.py:41
  112.3 0.0 copy-done.1
  112.3 2.8 %convolution_bitcast_fusion = f32[1024,256]{0,1:T(8,128)} fusion(f32[16,1024]{1,0:T(8,128)S(1)} %copy-done.1, f32[16,256]{1,0:T(8,128)} %reduce-scatter.5.cloned.1.call-done), kind=kOutput, calls=%fused_computation.1 | convolution fusion | flops 50335744 | bytes 1130496 | tf_op jit(solution)/shard_map/dot_general | solution.py:55
  115.1 0.0 all-reduce.2.cloned.1.call-update
  115.1 133.1 %all-reduce.2.cloned.1.call-done = f32[1024,256]{0,1:T(8,128)} async-done(((f32[1024,256]{0,1:T(8,128)}), f32[1024,256]{0,1:T(8,128)}) %all-reduce.2.cloned.1.call-update) | async-done | bytes 1048592 | tf_op jit(solution)/shard_map/psum | solution.py:62
  248.2 0.0 copy-done.2
  248.2 0.0 copy-done.6
  248.2 2.8 %fusion.3 = f32[16,256]{1,0:T(8,128)} fusion(f32[16,256]{1,0:T(8,128)S(1)} %copy-done.3, f32[16,1024]{1,0:T(8,128)S(1)} %copy-done.1, f32[1024,256]{0,1:T(8,128)} %all-reduce.2.cloned.1.call-done, f32[1024]{0:T(1024)S(1)} %copy-done.6, f32[16,256]{1,0:T(8,128)S(1)} %copy-done.2), kind=kOutput, calls=%fused_computation.8 | convolution fusion | flops 50610176 | bytes 1167360 | tf_op jit(solution)/shard_map/dot_general | solution.py:63
  (10 shorter events, 0.0 us)
Async XLA Ops:
  6.5 19.4 %copy-start = (f32[256,128]{1,0:T(8,128)S(1)}, f32[256,128]{1,0:T(8,128)}, u32[]{:S(2)}) copy-start(f32[256,128]{1,0:T(8,128)} %param.7) | copy-start | bytes 393220
  6.5 0.7 copy-start.7
  6.5 10.6 %copy-start.4 = (f32[16,1024]{1,0:T(8,128)S(1)}, f32[16,1024]{1,0:T(8,128)}, u32[]{:S(2)}) copy-start(f32[16,1024]{1,0:T(8,128)} %param.10) | copy-start | bytes 196612
  6.5 67.8 %reduce-scatter.7.cloned.1.call-start = ((), (), s32[]{:S(2)}) async-start(), calls=%async_computation.4 | async-start | bytes 147456
  43.7 0.9 copy-start.5
  43.7 68.6 %reduce-scatter.5.cloned.1.call-start = ((), (), s32[]{:S(2)}) async-start(), calls=%async_computation.2 | async-start | bytes 81920 | tf_op jit(solution)/shard_map/reduce_scatter | solution.py:41
  89.9 22.4 %copy-start.1 = (f32[16,1024]{1,0:T(8,128)S(1)}, f32[16,1024]{1,0:T(8,128)}, u32[]{:S(2)}) copy-start(f32[16,1024]{1,0:T(8,128)} %param.12) | copy-start | bytes 196612
  89.9 158.3 %all-reduce.2.cloned.1.call-start = ((), (), s32[]{:S(2)}) async-start(), calls=%async_computation.3 | async-start | bytes 2097152 | tf_op jit(solution)/shard_map/psum | solution.py:62
  115.1 133.2 %copy-start.2 = (f32[16,256]{1,0:T(8,128)S(1)}, f32[16,256]{1,0:T(8,128)}, u32[]{:S(2)}) copy-start(f32[16,256]{1,0:T(8,128)} %reduce-scatter.5.cloned.1.call-done) | copy-start | bytes 49156
  115.1 133.2 %copy-start.3 = (f32[16,256]{1,0:T(8,128)S(1)}, f32[16,256]{1,0:T(8,128)}, u32[]{:S(2)}) copy-start(f32[16,256]{1,0:T(8,128)} %param.11) | copy-start | bytes 49156
  115.1 133.2 %copy-start.6 = (f32[1024]{0:T(1024)S(1)}, f32[1024]{0:T(1024)}, u32[]{:S(2)}) copy-start(f32[1024]{0:T(1024)} %param.13) | copy-start | bytes 12292
Sparse Core Ops, SparseCore 0:
  43.8 30.4 reduce-scatter.6
  90.1 22.1 reduce-scatter.4
  117.5 130.6 all-reduce.1
where the time goes:
time: 258 us
  waiting for transfers between devices  185 us (72%)
  blocking collectives  47.8 us (19%)
  between operations  13.2 us (5%)
  matrix products  8.16 us (3%)
    psum x1, waiting for transfers between devices, on_device(): coords = lax.psum(local_coords, ('batch', 'centre'))  133 us
    unnamed x4, waiting for transfers between devices  29.7 us
    reduce_scatter x1, waiting for transfers between devices, on_device(): lax.psum_scatter(lax.dot_general(kernel, residual, (((0,), (0,)), ((), ()...  22.3 us
    all_gather x1, blocking collectives, on_device(): batch_x = lax.all_gather(picked, 'centre', axis=1, tiled=True)  15.2 us
    all_gather x1, blocking collectives, on_device(): lax.all_gather(columns - own_targets, 'centre', axis=1, tiled=True)  13.9 us
    all_gather x1, blocking collectives, on_device(): crows = lax.all_gather(coeffs, 'batch', axis=0, tiled=True)  9.88 us
    all_gather x1, blocking collectives, on_device(): zrows = lax.all_gather(centres, 'batch', axis=0, tiled=True)  8.8 us
  transfers between devices with their start and end apart: 3, of which 3 were waited for; matrix products, arithmetic and copies ran while one was open for 0% of the time, Pallas kernels for 0%

commit v1 on v0

--- a/solution.py
+++ b/solution.py
@@ -2,6 +2,11 @@
 import jax.numpy as jnp
 from jax import lax
 from jax.sharding import PartitionSpec as P
+
+
+def gather_and_add(x, axis):
+    parts = lax.all_gather(x, axis)
+    return jnp.sum(parts, axis=0)
 
 
 def on_device(pool, sample_index, targets, centres, coeffs, eigvecs, eigscale):
@@ -59,7 +64,7 @@
         precision=highest,
         preferred_element_type=jnp.float32,
     )
-    coords = lax.psum(local_coords, ("batch", "centre"))
+    coords = gather_and_add(local_coords, ("batch", "centre"))
     correction = jnp.dot(
         eigvecs, eigscale[:, None] * coords, precision=highest, preferred_element_type=jnp.float32
     )

time: 258 us -> 356 us (1.38)
  waiting for transfers between devices: 185 us -> 248 us
  local copies, waits for them, and re-layouts: 1.63 us -> 30.4 us
  other arithmetic: 1.54 us -> 9.72 us
    all_gather x0 -> x1, waiting for transfers between devices: none -> 196 us  [gather_and_add(): parts = lax.all_gather(x, axis)]
    psum x1 -> x0, waiting for transfers between devices: 133 us -> none  [on_device(): coords = lax.psum(local_coords, ('batch', 'centre'))]
    unnamed x17 -> x14, local copies, waits for them, and re-layouts: 0.91 us -> 28.9 us
    reduce_sum x0 -> x1, other arithmetic: none -> 7.55 us  [gather_and_add(): return jnp.sum(parts, axis=0)]
where the time goes in v1:
time: 356 us
  waiting for transfers between devices  248 us (70%)
  blocking collectives  47.8 us (13%)
  local copies, waits for them, and re-layouts  30.4 us (9%)
  between operations  13.2 us (4%)
  other arithmetic  9.72 us (3%)
  matrix products  7.03 us (2%)
    all_gather x1, waiting for transfers between devices, gather_and_add(): parts = lax.all_gather(x, axis)  196 us
    unnamed x4, waiting for transfers between devices  29.7 us
    unnamed x14, local copies, waits for them, and re-layouts  28.9 us
    reduce_scatter x1, waiting for transfers between devices, on_device(): lax.psum_scatter(lax.dot_general(kernel, residual, (((0,), (0,)), ((), ()...  22.3 us
    all_gather x1, blocking collectives, on_device(): batch_x = lax.all_gather(picked, 'centre', axis=1, tiled=True)  15.2 us
    all_gather x1, blocking collectives, on_device(): lax.all_gather(columns - own_targets, 'centre', axis=1, tiled=True)  13.9 us
    all_gather x1, blocking collectives, on_device(): crows = lax.all_gather(coeffs, 'batch', axis=0, tiled=True)  9.87 us
    all_gather x1, blocking collectives, on_device(): zrows = lax.all_gather(centres, 'batch', axis=0, tiled=True)  8.79 us
  transfers between devices with their start and end apart: 3, of which 3 were waited for; matrix products, arithmetic and copies ran while one was open for 0% of the time, Pallas kernels for 0%

profile of v1, /device:TPU:0, one launch (start us, length us, event | category | flops | bytes accessed | tf_op | source)
XLA Modules:
  0.0 355.9 jit_solution(2019846585788553945)
XLA Ops:
  6.5 0.7 compare_and_fusion
  7.2 0.7 compare_select_fusion
  7.9 9.9 %all_gather.20 = f32[64,256]{1,0:T(8,128)S(1)} all-gather(f32[16,256]{1,0:T(8,128)} %param.11), channel_id=1, replica_groups=mesh['batch'=4,'centre'=8] {'batch'}, dimensions={0}, use_global_device_ids=true | all-gather | bytes 81920 | tf_op jit(solution)/shard_map/all_gather | solution.py:27
  17.8 8.8 %all_gather.19 = f32[64,1024]{1,0:T(8,128)S(1)} all-gather(f32[16,1024]{1,0:T(8,128)} %param.10), channel_id=1, replica_groups=mesh['batch'=4,'centre'=8] {'batch'}, dimensions={0}, use_global_device_ids=true | all-gather | bytes 327680 | tf_op jit(solution)/shard_map/all_gather | solution.py:26
  26.6 0.0 copy-done
  26.6 0.6 gather_fusion
  27.2 0.1 broadcast_select_fusion
  27.3 15.2 %all_gather.18 = f32[128,1024]{1,0:T(8,128)S(1)} all-gather(f32[128,128]{1,0:T(8,128)S(1)} %broadcast_select_fusion), channel_id=1, replica_groups=mesh['batch'=4,'centre'=8] {'centre'}, dimensions={1}, use_global_device_ids=true | all-gather | bytes 589824 | tf_op jit(solution)/shard_map/all_gather | solution.py:15
  42.5 0.7 fusion
  43.2 1.1 convolution_bitcast_fusion.1
  44.2 0.0 reduce-scatter.7.cloned.1.call-update
  44.3 0.0 reduce-scatter.5.cloned.1.call-start
  44.3 0.9 constant_dynamic-slice_fusion
  45.2 0.1 copy.15
  45.3 29.6 %reduce-scatter.7.cloned.1.call-done = f32[32,128]{1,0:T(8,128)} async-done(((f32[256,128]{1,0:T(8,128)}), f32[32,128]{1,0:T(8,128)}) %reduce-scatter.7.cloned.1.call-update) | async-done | bytes 16400
  74.9 0.7 fusion.6
  75.6 13.9 %all_gather.21 = f32[128,256]{0,1:T(8,128)S(1)} all-gather(f32[128,32]{0,1:T(8,128)S(1)} %fusion.6), channel_id=1, replica_groups=mesh['batch'=4,'centre'=8] {'centre'}, dimensions={1}, use_global_device_ids=true | all-gather | bytes 147456 | tf_op jit(solution)/shard_map/all_gather | solution.py:44
  89.6 0.9 fusion.10
  90.5 0.0 reduce-scatter.5.cloned.1.call-update
  90.5 0.0 all-gather.3.cloned.1.call-start
  90.6 22.3 %reduce-scatter.5.cloned.1.call-done = f32[16,256]{1,0:T(8,128)} async-done(((f32[64,256]{1,0:T(8,128)}), f32[16,256]{1,0:T(8,128)}) %reduce-scatter.5.cloned.1.call-update) | async-done | bytes 16400 | tf_op jit(solution)/shard_map/reduce_scatter | solution.py:46
  112.9 2.9 convolution_bitcast_fusion
  115.7 0.0 all-gather.3.cloned.1.call-update
  115.8 195.6 %all-gather.3.cloned.1.call-done = f32[32768,256]{0,1:T(8,128)} async-done(((f32[1024,256]{0,1:T(8,128)}), f32[32768,256]{0,1:T(8,128)}) %all-gather.3.cloned.1.call-update) | async-done | bytes 33554448 | tf_op jit(solution)/shard_map/all_gather | solution.py:8
  311.3 28.8 %copy.16 = f32[32,8,32,1024]{3,2,1,0:T(8,128)S(1)} copy(f32[32,8,32,1024]{3,1,2,0:T(8,128)} %bitcast.29) | data formatting | bytes 67108864
  340.1 0.0 copy-start.2
  340.2 0.0 copy-start.4
  340.2 0.0 copy-start.5
  340.2 7.6 %bitcast_reduce_fusion = f32[1024,256]{0,1:T(8,128)S(1)} fusion(f32[32,8,32,1024]{3,2,1,0:T(8,128)S(1)} %copy.16), kind=kLoop, calls=%fused_computation.1 | loop fusion | flops 8126464 | bytes 34603008 | tf_op jit(solution)/shard_map/reduce_sum | solution.py:9
  347.7 0.0 copy-done.2
  347.8 0.0 copy-done.3
  347.8 1.5 fusion.3
  (8 shorter events, 0.0 us)
Async XLA Ops:
  6.5 20.0 %copy-start = (f32[256,128]{1,0:T(8,128)S(1)}, f32[256,128]{1,0:T(8,128)}, u32[]{:S(2)}) copy-start(f32[256,128]{1,0:T(8,128)} %param.7) | copy-start | bytes 393220
  6.5 68.4 %reduce-scatter.7.cloned.1.call-start = ((), (), s32[]{:S(2)}) async-start(), calls=%async_computation.4 | async-start | bytes 147456
  44.3 68.6 %reduce-scatter.5.cloned.1.call-start = ((), (), s32[]{:S(2)}) async-start(), calls=%async_computation.2 | async-start | bytes 81920 | tf_op jit(solution)/shard_map/reduce_scatter | solution.py:46
  90.5 220.8 %all-gather.3.cloned.1.call-start = ((), (), s32[]{:S(2)}) async-start(), calls=%async_computation.3 | async-start | bytes 34603008 | tf_op jit(solution)/shard_map/all_gather | solution.py:8
  311.3 38.0 %copy-start.1 = (f32[256,128]{1,0:T(8,128)S(1)}, f32[256,128]{1,0:T(8,128)}, u32[]{:S(2)}) copy-start(f32[256,128]{1,0:T(8,128)} %param.7) | copy-start | bytes 393220
  340.1 7.6 %copy-start.2 = (f32[16,1024]{1,0:T(8,128)S(1)}, f32[16,1024]{1,0:T(8,128)}, u32[]{:S(2)}) copy-start(f32[16,1024]{1,0:T(8,128)} %param.12) | copy-start | bytes 196612
  340.2 7.6 %copy-start.3 = (f32[16,256]{1,0:T(8,128)S(1)}, f32[16,256]{1,0:T(8,128)}, u32[]{:S(2)}) copy-start(f32[16,256]{1,0:T(8,128)} %reduce-scatter.5.cloned.1.call-done) | copy-start | bytes 49156
  340.2 7.6 %copy-start.4 = (f32[16,256]{1,0:T(8,128)S(1)}, f32[16,256]{1,0:T(8,128)}, u32[]{:S(2)}) copy-start(f32[16,256]{1,0:T(8,128)} %param.11) | copy-start | bytes 49156
  340.2 7.6 %copy-start.5 = (f32[1024]{0:T(1024)S(1)}, f32[1024]{0:T(1024)}, u32[]{:S(2)}) copy-start(f32[1024]{0:T(1024)} %param.13) | copy-start | bytes 12292
Sparse Core Ops, SparseCore 0:
  44.4 30.4 reduce-scatter.6
  90.6 22.1 reduce-scatter.4
  115.9 195.3 all-gather.2

commit v2 on v0

--- a/solution.py
+++ b/solution.py
@@ -59,7 +59,11 @@
         precision=highest,
         preferred_element_type=jnp.float32,
     )
-    coords = lax.psum(local_coords, ("batch", "centre"))
+
+    def lift_the_record(vec):
+        return lax.psum(lax.psum(vec, "centre"), "batch")
+
+    coords = lift_the_record(local_coords)
     correction = jnp.dot(
         eigvecs, eigscale[:, None] * coords, precision=highest, preferred_element_type=jnp.float32
     )

time: 258 us -> 239 us (0.926)
  waiting for transfers between devices: 185 us -> 166 us
    psum x1 -> x2, waiting for transfers between devices: 133 us -> 114 us  [lift_the_record(): return lax.psum(lax.psum(vec, 'centre'), 'batch')]
    unnamed x4 -> x5, waiting for transfers between devices: 29.7 us -> 29.7 us
  transfers between devices with their start and end apart: 3 -> 4, of which waited for: 3 -> 4; matrix products, arithmetic and copies ran while one was open for 0% -> 0% of each run, Pallas kernels for 0% -> 0%
where the time goes in v2:
time: 239 us; the launch traced here: 238 us
  waiting for transfers between devices  166 us (69%)
  blocking collectives  47.8 us (20%)
  between operations  13.2 us (6%)
  matrix products  8.16 us (3%)
    psum x2, waiting for transfers between devices, lift_the_record(): return lax.psum(lax.psum(vec, 'centre'), 'batch')  114 us
    unnamed x5, waiting for transfers between devices  29.7 us
    reduce_scatter x1, waiting for transfers between devices, on_device(): lax.psum_scatter(lax.dot_general(kernel, residual, (((0,), (0,)), ((), ()...  22.3 us
    all_gather x1, blocking collectives, on_device(): batch_x = lax.all_gather(picked, 'centre', axis=1, tiled=True)  15.2 us
    all_gather x1, blocking collectives, on_device(): lax.all_gather(columns - own_targets, 'centre', axis=1, tiled=True)  13.9 us
    all_gather x1, blocking collectives, on_device(): crows = lax.all_gather(coeffs, 'batch', axis=0, tiled=True)  9.88 us
    all_gather x1, blocking collectives, on_device(): zrows = lax.all_gather(centres, 'batch', axis=0, tiled=True)  8.8 us
  transfers between devices with their start and end apart: 4, of which 4 were waited for; matrix products, arithmetic and copies ran while one was open for 0% of the time, Pallas kernels for 0%

profile of v2, /device:TPU:0, one launch (start us, length us, event | category | flops | bytes accessed | tf_op | source)
XLA Modules:
  0.0 238.3 jit_solution(14141898400161874432)
XLA Ops:
  6.5 0.0 copy-start
  6.5 0.0 reduce-scatter.7.cloned.1.call-start
  6.5 0.7 compare_and_fusion
  7.3 0.0 copy-done.7
  7.3 9.9 %all_gather.14 = f32[64,256]{1,0:T(8,128)S(1)} all-gather(f32[16,256]{1,0:T(8,128)} %param.11), channel_id=1, replica_groups=mesh['batch'=4,'centre'=8] {'batch'}, dimensions={0}, use_global_device_ids=true | all-gather | bytes 81920 | tf_op jit(solution)/shard_map/all_gather | solution.py:22
  17.2 8.8 %all_gather.13 = f32[64,1024]{1,0:T(8,128)S(1)} all-gather(f32[16,1024]{1,0:T(8,128)S(1)} %copy-done.4), channel_id=1, replica_groups=mesh['batch'=4,'centre'=8] {'batch'}, dimensions={0}, use_global_device_ids=true | all-gather | bytes 327680 | tf_op jit(solution)/shard_map/all_gather | solution.py:21
  26.0 0.6 gather_fusion
  26.6 0.1 broadcast_select_fusion
  26.7 15.2 %all_gather.12 = f32[128,1024]{1,0:T(8,128)S(1)} all-gather(f32[128,128]{1,0:T(8,128)S(1)} %broadcast_select_fusion), channel_id=1, replica_groups=mesh['batch'=4,'centre'=8] {'centre'}, dimensions={1}, use_global_device_ids=true | all-gather | bytes 589824 | tf_op jit(solution)/shard_map/all_gather | solution.py:10
  41.9 0.7 fusion
  42.6 1.1 convolution_bitcast_fusion.1
  43.7 0.0 reduce-scatter.7.cloned.1.call-update
  43.7 0.0 reduce-scatter.5.cloned.1.call-start
  43.7 0.8 copy-done.5
  44.6 0.1 constant_dynamic-slice_fusion
  44.6 0.1 copy.15
  44.7 29.6 %reduce-scatter.7.cloned.1.call-done = f32[32,128]{1,0:T(8,128)} async-done(((f32[256,128]{1,0:T(8,128)}), f32[32,128]{1,0:T(8,128)}) %reduce-scatter.7.cloned.1.call-update) | async-done | bytes 16400
  74.3 0.7 fusion.6
  75.1 13.9 %all_gather.15 = f32[128,256]{0,1:T(8,128)S(1)} all-gather(f32[128,32]{0,1:T(8,128)S(1)} %fusion.6), channel_id=1, replica_groups=mesh['batch'=4,'centre'=8] {'centre'}, dimensions={1}, use_global_device_ids=true | all-gather | bytes 147456 | tf_op jit(solution)/shard_map/all_gather | solution.py:39
  89.0 0.9 fusion.10
  89.9 0.0 reduce-scatter.5.cloned.1.call-update
  89.9 0.0 all-reduce.3.cloned.1.call-start
  90.0 22.3 %reduce-scatter.5.cloned.1.call-done = f32[16,256]{1,0:T(8,128)} async-done(((f32[64,256]{1,0:T(8,128)}), f32[16,256]{1,0:T(8,128)}) %reduce-scatter.5.cloned.1.call-update) | async-done | bytes 16400 | tf_op jit(solution)/shard_map/reduce_scatter | solution.py:41
  112.3 2.8 %convolution_bitcast_fusion = f32[1024,256]{0,1:T(8,128)} fusion(f32[16,1024]{1,0:T(8,128)S(1)} %copy-done.1, f32[16,256]{1,0:T(8,128)} %reduce-scatter.5.cloned.1.call-done), kind=kOutput, calls=%fused_computation.1 | convolution fusion | flops 50335744 | bytes 1130496 | tf_op jit(solution)/shard_map/dot_general | solution.py:55
  115.1 0.0 all-reduce.3.cloned.1.call-update
  115.1 0.0 all-reduce.5.cloned.1.call-start
  115.2 59.3 %all-reduce.3.cloned.1.call-done = f32[1024,256]{0,1:T(8,128)} async-done(((f32[1024,256]{0,1:T(8,128)}), f32[1024,256]{0,1:T(8,128)}) %all-reduce.3.cloned.1.call-update) | async-done | bytes 1048592 | tf_op jit(solution)/shard_map/psum | solution.py:64
  174.5 0.0 all-reduce.5.cloned.1.call-update
  174.5 54.5 %all-reduce.5.cloned.1.call-done = f32[1024,256]{0,1:T(8,128)} async-done(((f32[1024,256]{0,1:T(8,128)}), f32[1024,256]{0,1:T(8,128)}) %all-reduce.5.cloned.1.call-update) | async-done | bytes 1048592 | tf_op jit(solution)/shard_map/psum | solution.py:64
  229.0 0.0 copy-done.2
  229.0 0.0 copy-done.6
  229.0 2.8 %fusion.3 = f32[16,256]{1,0:T(8,128)} fusion(f32[16,256]{1,0:T(8,128)S(1)} %copy-done.3, f32[16,1024]{1,0:T(8,128)S(1)} %copy-done.1, f32[1024,256]{0,1:T(8,128)} %all-reduce.5.cloned.1.call-done, f32[1024]{0:T(1024)S(1)} %copy-done.6, f32[16,256]{1,0:T(8,128)S(1)} %copy-done.2), kind=kOutput, calls=%fused_computation.8 | convolution fusion | flops 50610176 | bytes 1167360 | tf_op jit(solution)/shard_map/dot_general | solution.py:67
  (13 shorter events, 0.0 us)
Async XLA Ops:
  6.5 19.4 %copy-start = (f32[256,128]{1,0:T(8,128)S(1)}, f32[256,128]{1,0:T(8,128)}, u32[]{:S(2)}) copy-start(f32[256,128]{1,0:T(8,128)} %param.7) | copy-start | bytes 393220
  6.5 0.7 copy-start.7
  6.5 10.6 %copy-start.4 = (f32[16,1024]{1,0:T(8,128)S(1)}, f32[16,1024]{1,0:T(8,128)}, u32[]{:S(2)}) copy-start(f32[16,1024]{1,0:T(8,128)} %param.10) | copy-start | bytes 196612
  6.5 67.8 %reduce-scatter.7.cloned.1.call-start = ((), (), s32[]{:S(2)}) async-start(), calls=%async_computation.5 | async-start | bytes 147456
  43.7 0.9 copy-start.5
  43.7 68.6 %reduce-scatter.5.cloned.1.call-start = ((), (), s32[]{:S(2)}) async-start(), calls=%async_computation.2 | async-start | bytes 81920 | tf_op jit(solution)/shard_map/reduce_scatter | solution.py:41
  89.9 22.4 %copy-start.1 = (f32[16,1024]{1,0:T(8,128)S(1)}, f32[16,1024]{1,0:T(8,128)}, u32[]{:S(2)}) copy-start(f32[16,1024]{1,0:T(8,128)} %param.12) | copy-start | bytes 196612
  89.9 84.5 %all-reduce.3.cloned.1.call-start = ((), (), s32[]{:S(2)}) async-start(), calls=%async_computation.3 | async-start | bytes 2097152 | tf_op jit(solution)/shard_map/psum | solution.py:64
  115.1 113.9 %all-reduce.5.cloned.1.call-start = ((), (), s32[]{:S(2)}) async-start(), calls=%async_computation.4 | async-start | bytes 2097152 | tf_op jit(solution)/shard_map/psum | solution.py:64
  174.5 54.5 %copy-start.2 = (f32[16,256]{1,0:T(8,128)S(1)}, f32[16,256]{1,0:T(8,128)}, u32[]{:S(2)}) copy-start(f32[16,256]{1,0:T(8,128)} %reduce-scatter.5.cloned.1.call-done) | copy-start | bytes 49156
  174.5 54.5 %copy-start.3 = (f32[16,256]{1,0:T(8,128)S(1)}, f32[16,256]{1,0:T(8,128)}, u32[]{:S(2)}) copy-start(f32[16,256]{1,0:T(8,128)} %param.11) | copy-start | bytes 49156
  174.5 54.5 %copy-start.6 = (f32[1024]{0:T(1024)S(1)}, f32[1024]{0:T(1024)}, u32[]{:S(2)}) copy-start(f32[1024]{0:T(1024)} %param.13) | copy-start | bytes 12292
Sparse Core Ops, SparseCore 0:
  43.8 30.4 reduce-scatter.6
  90.1 22.1 reduce-scatter.4
  115.2 59.2 all-reduce.2
  177.4 51.5 all-reduce.4
